TPU v7x, 32 devices: a whole 2x2x4 slice. The times are simulated.
32 devices in a mesh: dp: 8 (over z, core), mp: 4 (over y, x).
Axes of the slice: x: 2, y: 2, z: 4, core: 2. Of those that a mesh axis runs over, the one named last changes fastest.
Arguments:
- grad_parts: bfloat16 [8, 64, 256, 256], P('dp', 'mp'), may hold values from -0.25 to 0.25
- left_stats: float32 [8, 4, 4, 256, 256], P('dp', 'mp'), may hold values from -6 to 6
- right_stats: float32 [8, 4, 4, 256, 256], P('dp', 'mp'), may hold values from -6 to 6
- left_root: bfloat16 [8, 4, 4, 256, 256], P('dp', 'mp'), may hold values from -4 to 4
- right_root: bfloat16 [8, 4, 4, 256, 256], P('dp', 'mp'), may hold values from -4 to 4
- owners: int32 [64], replicated, may hold values from 0 to 3, as said below
Outputs:
- direction: bfloat16 [64, 256, 256], P('mp')
- left_updated: float32 [8, 4, 4, 256, 256], P('dp', 'mp')
- right_updated: float32 [8, 4, 4, 256, 256], P('dp', 'mp')
Inputs may be any that keep to these rules, and one draw needn't show every extreme that they name: The blocks b with the same b // 2 have distinct owners. Among the blocks of one row, no owner is named more than 4 times, and in every row some owner is named exactly 4 times.
All inputs are finite; a program needn't handle non-finite values.
Results may differ from a plain program's by a relative error of at most 0.02.
Values may be sent and summed in bfloat16 or wider, within the bound.
A program may use at most 64 MiB of HBM per device.

v0:
```python
import jax
import jax.numpy as jnp
from jax import lax
from jax.sharding import PartitionSpec as P


def per_device(grad_parts, left_stats, right_stats, left_root, right_root, owners):
    dp_count = lax.axis_size("dp")
    mp_count = lax.axis_size("mp")
    dp_index = lax.axis_index("dp")
    mp_index = lax.axis_index("mp")
    per_shard = grad_parts.shape[1]
    held_count = per_shard // dp_count
    slots_count = left_stats.shape[2]
    total_blocks = owners.shape[0]
    block_ids = jnp.arange(total_blocks, dtype=jnp.int32)
    row_of = block_ids % per_shard // held_count
    same_owner = owners[:, None] == owners[None, :]
    before = block_ids[None, :] < block_ids[:, None]
    slot_of = jnp.sum(
        ((row_of[:, None] == row_of[None, :]) & same_owner & before).astype(jnp.int32), axis=1
    )
    row_pos = jnp.arange(mp_count * held_count, dtype=jnp.int32)
    row_ids = row_pos // held_count * per_shard + dp_index * held_count + row_pos % held_count
    row_owner = jnp.take(owners, row_ids)
    row_slot = jnp.take(slot_of, row_ids)
    slot_ids = jnp.arange(slots_count, dtype=jnp.int32)
    mine_in = (row_owner[None, :] == mp_index) & (row_slot[None, :] == slot_ids[:, None])
    local_ids = (
        mp_index * per_shard + dp_index * held_count + jnp.arange(held_count, dtype=jnp.int32)
    )
    local_owner = jnp.take(owners, local_ids)
    summed = lax.psum(grad_parts[0], "dp").astype(jnp.float32)
    shares = lax.dynamic_slice_in_dim(summed, dp_index * held_count, held_count, 0)
    held_blocks = shares.astype(jnp.bfloat16)
    targets = jnp.arange(mp_count, dtype=jnp.int32)
    send_map = (local_owner[None, :] == targets[:, None]).astype(jnp.bfloat16)
    row_holder = row_pos // held_count
    receive_map = jnp.any(
        mine_in[:, :, None] & (row_holder[None, :, None] == targets[None, None, :]), axis=1
    ).astype(jnp.bfloat16)
    packed = jnp.einsum(
        "qj,jxy->qxy", send_map, held_blocks, preferred_element_type=jnp.float32
    ).astype(jnp.bfloat16)
    arrived = lax.all_to_all(packed, "mp", split_axis=0, concat_axis=0, tiled=True)
    owned_grad = jnp.einsum(
        "sq,qxy->sxy", receive_map, arrived, preferred_element_type=jnp.float32
    ).astype(jnp.bfloat16)
    left_updated = left_stats[0, 0] + jnp.einsum(
        "sik,sjk->sij", owned_grad, owned_grad, preferred_element_type=jnp.float32
    )
    right_updated = right_stats[0, 0] + jnp.einsum(
        "ski,skj->sij", owned_grad, owned_grad, preferred_element_type=jnp.float32
    )
    half_step = jnp.einsum(
        "sik,skj->sij", left_root[0, 0], owned_grad, preferred_element_type=jnp.float32
    ).astype(jnp.bfloat16)
    precond = jnp.einsum(
        "sik,skj->sij", half_step, right_root[0, 0], preferred_element_type=jnp.float32
    ).astype(jnp.bfloat16)
    out_packed = jnp.einsum(
        "sq,sxy->qxy", receive_map, precond, preferred_element_type=jnp.float32
    ).astype(jnp.bfloat16)
    came_back = lax.all_to_all(out_packed, "mp", split_axis=0, concat_axis=0, tiled=True)
    returned = jnp.einsum(
        "qj,qxy->jxy", send_map, came_back, preferred_element_type=jnp.float32
    ).astype(jnp.bfloat16)
    direction = lax.all_gather(returned, "dp", axis=0, tiled=True)
    return (direction, left_updated[None, None], right_updated[None, None])


def solution(mesh):
    in_specs = (
        P("dp", "mp", None, None),
        P("dp", "mp", None, None, None),
        P("dp", "mp", None, None, None),
        P("dp", "mp", None, None, None),
        P("dp", "mp", None, None, None),
        P(),
    )
    out_specs = (
        P("mp", None, None),
        P("dp", "mp", None, None, None),
        P("dp", "mp", None, None, None),
    )
    return jax.shard_map(
        per_device, mesh=mesh, in_specs=in_specs, out_specs=out_specs, check_vma=False
    )
```

profile of v0, /device:TPU:0, one launch (start us, length us, event | category | flops | bytes accessed | tf_op | source)
XLA Modules:
  0.0 142.9 jit_solution(12366330903584625655)
XLA Ops:
  7.2 0.0 copy-start
  7.2 0.0 all-reduce.2.cloned.1.call-start
  7.2 4.1 %copy.61 = bf16[1,16,256,256]{3,1,2,0:T(8,128)(2,1)} copy(bf16[1,16,256,256]{3,2,1,0:T(8,128)(2,1)} %param.8) | data formatting | bytes 4194304 | tf_op args[0]
  11.4 0.0 copy-start.1
  11.4 0.0 all-reduce.2.cloned.1.call-update
  11.4 0.6 copy-done.1
  12.0 0.2 convert_reduce_fusion
  12.2 0.6 gather_fusion.1
  12.9 0.6 gather_fusion.2
  13.5 0.6 gather_fusion
  14.2 65.2 %all-reduce.2.cloned.1.call-done = bf16[16,256,256]{2,0,1:T(8,128)(2,1)} async-done(((bf16[16,256,256]{2,0,1:T(8,128)(2,1)}), bf16[16,256,256]{2,0,1:T(8,128)(2,1)}) %all-reduce.2.cloned.1.call-update) | async-done | bytes 2097168 | tf_op jit(solution)/shard_map/psum | solution.py:33
  79.4 1.8 %convolution_convert_fusion.4 = bf16[4,256,256]{2,0,1:T(4,128)(2,1)S(1)} fusion(bf16[16,256,256]{2,0,1:T(8,128)(2,1)} %all-reduce.2.cloned.1.call-done, s32[]{:T(128)S(6)} %select_n.90, s32[2]{0:T(128)S(1)} %and_select_fusion.4), kind=kOutput, calls=%fused_computation.12 | convolution fusion | flops 1572872 | bytes 786444 | tf_op jit(solution)/shard_map/qj,jxy->qxy/dot_general | solution.py:42
  81.2 0.0 copy-start.3
  81.2 0.9 copy.34
  82.1 3.6 %all-to-all-start = ((bf16[4,256,256]{2,1,0:T(8,128)(2,1)}), bf16[4,256,256]{2,1,0:T(8,128)(2,1)S(1)}, u32[]{:S(2)}, u32[]{:S(2)}) async-start(bf16[4,256,256]{2,1,0:T(8,128)(2,1)} %copy.34), calls=%async_computation | async-start | bytes 1048576 | tf_op jit(solution)/shard_map/all_to_all | solution.py:45
  85.8 0.0 all-gather.2.cloned.1.call-start
  85.8 0.2 and_reduce_fusion
  85.9 6.5 %all-to-all-done = bf16[4,256,256]{2,1,0:T(8,128)(2,1)S(1)} async-done(((bf16[4,256,256]{2,1,0:T(8,128)(2,1)}), bf16[4,256,256]{2,1,0:T(8,128)(2,1)S(1)}, u32[]{:S(2)}, u32[]{:S(2)}) %all-to-all-start) | async-done | bytes 524320 | tf_op jit(solution)/shard_map/all_to_all | solution.py:45
  92.5 0.5 convolution_convert_fusion.3
  93.0 0.3 copy.36
  93.3 0.0 copy-done
  93.3 0.0 copy-done.3
  93.3 0.6 convolution_convert_fusion.1
  93.9 0.6 convolution_convert_fusion
  94.5 0.1 copy.40
  94.6 9.7 %all_to_all.10 = bf16[4,256,256]{2,1,0:T(8,128)(2,1)S(1)} all-to-all(bf16[4,256,256]{2,1,0:T(8,128)(2,1)S(1)} %copy.40), channel_id=1, replica_groups=mesh['dp'=8,'mp'=4] {'mp'}, dimensions={0} | all-to-all | bytes 1048576 | tf_op jit(solution)/shard_map/all_to_all | solution.py:64
  104.3 0.0 copy-start.2
  104.3 0.5 convolution_convert_fusion.5
  104.8 0.7 copy.42
  105.5 0.0 all-gather.2.cloned.1.call-update
  105.6 2.5 %fusion.1 = f32[1,1,4,256,256]{4,3,2,1,0:T(8,128)} fusion(f32[1,1,4,256,256]{4,3,2,1,0:T(8,128)} %param.9, bf16[4,256,256]{2,0,1:T(4,128)(2,1)S(1)} %convolution_convert_fusion.3), kind=kOutput, calls=%fused_computation.7 | convolution fusion | flops 134479872 | bytes 2621440 | tf_op jit(solution)/shard_map/sik,sjk->sij/dot_general | solution.py:49
  108.1 0.0 copy-done.2
  108.1 1.3 fusion
  109.4 23.6 %all-gather.2.cloned.1.call-done = bf16[16,256,256]{2,1,0:T(8,128)(2,1)} async-done(((bf16[2,256,256]{2,1,0:T(8,128)(2,1)}), bf16[16,256,256]{2,1,0:T(8,128)(2,1)}) %all-gather.2.cloned.1.call-update) | async-done | bytes 2097168 | tf_op jit(solution)/shard_map/all_gather | solution.py:68
  132.9 3.1 %copy.64 = bf16[16,256,256]{2,1,0:T(8,128)(2,1)} copy(bf16[16,256,256]{2,1,0:T(8,128)(2,1)} %all-gather.2.cloned.1.call-done) | data formatting | bytes 4194304
  (11 shorter events, 0.1 us)
Async XLA Ops:
  7.2 86.1 %copy-start = (bf16[1,1,4,256,256]{4,3,2,1,0:T(8,128)(2,1)S(1)}, bf16[1,1,4,256,256]{4,3,2,1,0:T(8,128)(2,1)}, u32[]{:S(2)}) copy-start(bf16[1,1,4,256,256]{4,3,2,1,0:T(8,128)(2,1)} %param.12) | copy-start | bytes 1572868
  7.2 72.2 %all-reduce.2.cloned.1.call-start = ((), (), s32[]{:S(2)}) async-start(), calls=%async_computation.2 | async-start | bytes 4194304 | tf_op jit(solution)/shard_map/psum | solution.py:33
  11.4 0.7 copy-start.1
  81.2 12.1 %copy-start.3 = (bf16[1,1,4,256,256]{4,3,2,1,0:T(8,128)(2,1)S(1)}, bf16[1,1,4,256,256]{4,3,2,1,0:T(8,128)(2,1)}, u32[]{:S(2)}) copy-start(bf16[1,1,4,256,256]{4,3,2,1,0:T(8,128)(2,1)} %param.11) | copy-start | bytes 1572868
  82.1 10.3 %all-to-all-start = ((bf16[4,256,256]{2,1,0:T(8,128)(2,1)}), bf16[4,256,256]{2,1,0:T(8,128)(2,1)S(1)}, u32[]{:S(2)}, u32[]{:S(2)}) async-start(bf16[4,256,256]{2,1,0:T(8,128)(2,1)} %copy.34), calls=%async_computation | async-start | bytes 1048576 | tf_op jit(solution)/shard_map/all_to_all | solution.py:45
  85.8 47.2 %all-gather.2.cloned.1.call-start = ((), (), s32[]{:S(2)}) async-start(), calls=%async_computation.3 | async-start | bytes 2359296 | tf_op jit(solution)/shard_map/all_gather | solution.py:68
  104.3 3.9 %copy-start.2 = (f32[1,1,4,256,256]{4,3,2,1,0:T(8,128)S(1)}, f32[1,1,4,256,256]{4,3,2,1,0:T(8,128)}, u32[]{:S(2)}) copy-start(f32[1,1,4,256,256]{4,3,2,1,0:T(8,128)} %param.10) | copy-start | bytes 3145732
Sparse Core Ops, SparseCore 0:
  11.5 67.8 all-reduce.1
  105.7 27.2 all-gather.1
where the time goes:
time: 143 us
  waiting for transfers between devices  95.3 us (67%)
  between operations  14.2 us (10%)
  local copies, waits for them, and re-layouts  11.8 us (8%)
  blocking collectives  9.67 us (7%)
  matrix products  7.86 us (5%)
  starting transfers between devices  3.69 us (3%)
    psum x1, waiting for transfers between devices, per_device(): summed = lax.psum(grad_parts[0], 'dp').astype(jnp.float32)  65.2 us
    all_gather x1, waiting for transfers between devices, per_device(): direction = lax.all_gather(returned, 'dp', axis=0, tiled=True)  23.6 us
    all_to_all x1, blocking collectives, per_device(): lax.all_to_all(out_packed, 'mp', split_axis=0, concat_axis=0, tiled=True)  9.67 us
    unnamed x10, local copies, waits for them, and re-layouts  7.84 us
    all_to_all x1, waiting for transfers between devices, per_device(): lax.all_to_all(packed, 'mp', split_axis=0, concat_axis=0, tiled=True)  6.52 us
    all_to_all x1, starting transfers between devices, per_device(): lax.all_to_all(packed, 'mp', split_axis=0, concat_axis=0, tiled=True)  3.65 us
  transfers between devices with their start and end apart: 3, of which 3 were waited for; matrix products, arithmetic and copies ran while one was open for 4% of the time, Pallas kernels for 0%

commit v1 on v0

--- a/solution.py
+++ b/solution.py
@@ -30,7 +30,7 @@
         mp_index * per_shard + dp_index * held_count + jnp.arange(held_count, dtype=jnp.int32)
     )
     local_owner = jnp.take(owners, local_ids)
-    summed = lax.psum(grad_parts[0], "dp").astype(jnp.float32)
+    summed = jnp.sum(lax.all_gather(grad_parts[0], "dp"), 0).astype(jnp.float32)
     shares = lax.dynamic_slice_in_dim(summed, dp_index * held_count, held_count, 0)
     held_blocks = shares.astype(jnp.bfloat16)
     targets = jnp.arange(mp_count, dtype=jnp.int32)

time: 143 us -> 237 us (1.66)
  waiting for transfers between devices: 95.3 us -> 185 us
  other arithmetic: 0.42 us -> 9.57 us
  local copies, waits for them, and re-layouts: 11.8 us -> 7.07 us
    all_gather x0 -> x1, waiting for transfers between devices: none -> 153 us  [per_device(): summed = jnp.sum(lax.all_gather(grad_parts[0], 'dp'), 0).astype(jnp.float32)]
    psum x1 -> x0, waiting for transfers between devices: 65.2 us -> none  [per_device(): summed = lax.psum(grad_parts[0], 'dp').astype(jnp.float32)]
    reduce_sum x0 -> x1, other arithmetic: none -> 9.14 us  [per_device(): summed = jnp.sum(lax.all_gather(grad_parts[0], 'dp'), 0).astype(jnp.float32)]
    unnamed x10 -> x9, local copies, waits for them, and re-layouts: 7.84 us -> 3.12 us
  transfers between devices with their start and end apart: 3 -> 3, of which waited for: 3 -> 3; matrix products, arithmetic and copies ran while one was open for 4% -> 3% of each run, Pallas kernels for 0% -> 0%
where the time goes in v1:
time: 237 us; the launch traced here: 236 us
  waiting for transfers between devices  185 us (78%)
  between operations  14.2 us (6%)
  blocking collectives  10.6 us (4%)
  other arithmetic  9.57 us (4%)
  local copies, waits for them, and re-layouts  7.07 us (3%)
  matrix products  6.63 us (3%)
  starting transfers between devices  3.69 us (2%)
    all_gather x1, waiting for transfers between devices, per_device(): summed = jnp.sum(lax.all_gather(grad_parts[0], 'dp'), 0).astype(jnp.float32)  153 us
    all_gather x1, waiting for transfers between devices, per_device(): direction = lax.all_gather(returned, 'dp', axis=0, tiled=True)  22.2 us
    all_to_all x1, blocking collectives, per_device(): lax.all_to_all(out_packed, 'mp', split_axis=0, concat_axis=0, tiled=True)  10.6 us
    reduce_sum x1, other arithmetic, per_device(): summed = jnp.sum(lax.all_gather(grad_parts[0], 'dp'), 0).astype(jnp.float32)  9.14 us
    all_to_all x1, waiting for transfers between devices, per_device(): lax.all_to_all(packed, 'mp', split_axis=0, concat_axis=0, tiled=True)  8.33 us
  transfers between devices with their start and end apart: 3, of which 3 were waited for; matrix products, arithmetic and copies ran while one was open for 3% of the time, Pallas kernels for 0%

profile of v1, /device:TPU:0, one launch (start us, length us, event | category | flops | bytes accessed | tf_op | source)
XLA Modules:
  0.0 236.2 jit_solution(12910935962060760346)
XLA Ops:
  7.2 0.0 copy-start
  7.2 0.0 copy-start.1
  7.2 0.0 all-gather.3.cloned.1.call-start
  7.2 0.7 all-gather.3.cloned.1.call-update
  8.0 0.0 copy-done.1
  8.0 0.6 gather_fusion
  8.6 0.6 gather_fusion.1
  9.3 0.2 convert_reduce_fusion
  9.5 0.6 gather_fusion.2
  10.2 153.3 %all-gather.3.cloned.1.call-done = bf16[8,16,256,256]{3,2,1,0:T(8,128)(2,1)} async-done(((bf16[1,16,256,256]{3,2,1,0:T(8,128)(2,1)}), bf16[8,16,256,256]{3,2,1,0:T(8,128)(2,1)}) %all-gather.3.cloned.1.call-update) | async-done | bytes 16777232 | tf_op jit(solution)/shard_map/all_gather | solution.py:33
  163.4 9.1 %reduce_sum.22 = bf16[16,256,256]{2,1,0:T(8,128)(2,1)S(1)} reduce(bf16[8,16,256,256]{3,2,1,0:T(8,128)(2,1)} %all-gather.3.cloned.1.call-done, bf16[]{:T(256)} %constant.100.clone.1), dimensions={0}, to_apply=%region_2.4 | reduce | flops 7340032 | bytes 18874370 | tf_op jit(solution)/shard_map/reduce_sum | solution.py:33
  172.6 0.6 convolution_convert_fusion.4
  173.2 0.0 copy-start.3
  173.2 0.9 copy.47
  174.1 3.6 %all-to-all-start = ((bf16[4,256,256]{2,1,0:T(8,128)(2,1)}), bf16[4,256,256]{2,1,0:T(8,128)(2,1)S(1)}, u32[]{:S(2)}, u32[]{:S(2)}) async-start(bf16[4,256,256]{2,1,0:T(8,128)(2,1)} %copy.47), calls=%async_computation | async-start | bytes 1048576 | tf_op jit(solution)/shard_map/all_to_all | solution.py:45
  177.7 0.0 all-gather.5.cloned.1.call-start
  177.8 0.2 and_reduce_fusion
  177.9 8.3 %all-to-all-done = bf16[4,256,256]{2,1,0:T(8,128)(2,1)S(1)} async-done(((bf16[4,256,256]{2,1,0:T(8,128)(2,1)}), bf16[4,256,256]{2,1,0:T(8,128)(2,1)S(1)}, u32[]{:S(2)}, u32[]{:S(2)}) %all-to-all-start) | async-done | bytes 524320 | tf_op jit(solution)/shard_map/all_to_all | solution.py:45
  186.2 0.5 convolution_convert_fusion.3
  186.8 0.3 copy.49
  187.1 0.0 copy-done
  187.1 0.0 copy-done.3
  187.1 0.6 convolution_convert_fusion.1
  187.7 0.6 convolution_convert_fusion
  188.3 0.1 copy.53
  188.4 10.6 %all_to_all.10 = bf16[4,256,256]{2,1,0:T(8,128)(2,1)S(1)} all-to-all(bf16[4,256,256]{2,1,0:T(8,128)(2,1)S(1)} %copy.53), channel_id=1, replica_groups=mesh['dp'=8,'mp'=4] {'mp'}, dimensions={0} | all-to-all | bytes 1048576 | tf_op jit(solution)/shard_map/all_to_all | solution.py:64
  198.9 0.0 copy-start.2
  198.9 0.5 convolution_convert_fusion.5
  199.5 0.7 copy.55
  200.2 0.0 all-gather.5.cloned.1.call-update
  200.2 2.5 %fusion.1 = f32[1,1,4,256,256]{4,3,2,1,0:T(8,128)} fusion(f32[1,1,4,256,256]{4,3,2,1,0:T(8,128)} %param.9, bf16[4,256,256]{2,0,1:T(4,128)(2,1)S(1)} %convolution_convert_fusion.3), kind=kOutput, calls=%fused_computation.6 | convolution fusion | flops 134479872 | bytes 2621440 | tf_op jit(solution)/shard_map/sik,sjk->sij/dot_general | solution.py:49
  202.8 0.0 copy-done.2
  202.8 1.3 fusion
  204.1 22.2 %all-gather.5.cloned.1.call-done = bf16[16,256,256]{2,1,0:T(8,128)(2,1)} async-done(((bf16[2,256,256]{2,1,0:T(8,128)(2,1)}), bf16[16,256,256]{2,1,0:T(8,128)(2,1)}) %all-gather.5.cloned.1.call-update) | async-done | bytes 2097168 | tf_op jit(solution)/shard_map/all_gather | solution.py:68
  226.3 3.1 %copy.79 = bf16[16,256,256]{2,1,0:T(8,128)(2,1)} copy(bf16[16,256,256]{2,1,0:T(8,128)(2,1)} %all-gather.5.cloned.1.call-done) | data formatting | bytes 4194304
  (12 shorter events, 0.1 us)
Async XLA Ops:
  7.2 179.9 %copy-start = (bf16[1,1,4,256,256]{4,3,2,1,0:T(8,128)(2,1)S(1)}, bf16[1,1,4,256,256]{4,3,2,1,0:T(8,128)(2,1)}, u32[]{:S(2)}) copy-start(bf16[1,1,4,256,256]{4,3,2,1,0:T(8,128)(2,1)} %param.12) | copy-start | bytes 1572868
  7.2 0.8 copy-start.1
  7.2 156.2 %all-gather.3.cloned.1.call-start = ((), (), s32[]{:S(2)}) async-start(), calls=%async_computation.2 | async-start | bytes 18874368 | tf_op jit(solution)/shard_map/all_gather | solution.py:33
  173.2 13.9 %copy-start.3 = (bf16[1,1,4,256,256]{4,3,2,1,0:T(8,128)(2,1)S(1)}, bf16[1,1,4,256,256]{4,3,2,1,0:T(8,128)(2,1)}, u32[]{:S(2)}) copy-start(bf16[1,1,4,256,256]{4,3,2,1,0:T(8,128)(2,1)} %param.11) | copy-start | bytes 1572868
  174.1 12.2 %all-to-all-start = ((bf16[4,256,256]{2,1,0:T(8,128)(2,1)}), bf16[4,256,256]{2,1,0:T(8,128)(2,1)S(1)}, u32[]{:S(2)}, u32[]{:S(2)}) async-start(bf16[4,256,256]{2,1,0:T(8,128)(2,1)} %copy.47), calls=%async_computation | async-start | bytes 1048576 | tf_op jit(solution)/shard_map/all_to_all | solution.py:45
  177.7 48.5 %all-gather.5.cloned.1.call-start = ((), (), s32[]{:S(2)}) async-start(), calls=%async_computation.3 | async-start | bytes 2359296 | tf_op jit(solution)/shard_map/all_gather | solution.py:68
  198.9 3.9 %copy-start.2 = (f32[1,1,4,256,256]{4,3,2,1,0:T(8,128)S(1)}, f32[1,1,4,256,256]{4,3,2,1,0:T(8,128)}, u32[]{:S(2)}) copy-start(f32[1,1,4,256,256]{4,3,2,1,0:T(8,128)} %param.10) | copy-start | bytes 3145732
Sparse Core Ops, SparseCore 0:
  9.6 153.7 all-gather.2
  200.4 25.8 all-gather.4
